TPU v7x, 32 devices: a whole 2x2x4 slice. The times are simulated.
32 devices in a mesh: gx: 4 (over z), gy: 4 (over x, core), gz: 2 (over y).
Axes of the slice: x: 2, y: 2, z: 4, core: 2. Of those that a mesh axis runs over, the one named last changes fastest.
Arguments:
- x_a: bfloat16 [32, 8, 64, 256], P(None, 'gx', 'gy', 'gz'), may hold values from -12 to 12
- x_b: bfloat16 [32, 8, 64, 256], P(None, 'gx', 'gy', 'gz'), may hold values from -12 to 12
- w_first: bfloat16 [3, 3, 3, 32, 32], replicated, may hold values from -0.21875 to 0.21875
- w_second: bfloat16 [3, 3, 3, 32, 32], replicated, may hold values from -0.21875 to 0.21875
- gain_first: float32 [32], replicated, may hold values from 0.1 to 1.9
- bias_first: float32 [32], replicated, may hold values from -2 to 2
- gain_second: float32 [32], replicated, may hold values from 0.1 to 1.9
- bias_second: float32 [32], replicated, may hold values from -2 to 2
- grad_out: bfloat16 [32, 8, 64, 256], P(None, 'gx', 'gy', 'gz'), may hold values from -6 to 6
Outputs:
- y_a: bfloat16 [32, 8, 64, 256], P(None, 'gx', 'gy', 'gz')
- dx_b: bfloat16 [32, 8, 64, 256], P(None, 'gx', 'gy', 'gz')
- grad_w_first: float32 [3, 3, 3, 32, 32], replicated
- grad_w_second: float32 [3, 3, 3, 32, 32], replicated
- grad_norm: float32 [4, 32], replicated
All inputs are finite; a program needn't handle non-finite values.
Results may differ from a plain program's by a relative error of at most 0.0063.
Values may be sent and summed in bfloat16 or wider, within the bound.
No kernel may reach another device: no remote copies, remote signals or barrier semaphores. Data moves between devices by JAX's collectives and lax.ppermute only.
A program may use at most 128 MiB of HBM per device.

v0:
```python
import math
import jax
import jax.numpy as jnp
from jax import lax
from jax.sharding import PartitionSpec as P

EPSILON = 1e-05


def extended(block, sides, width):
    for axis, dim in sides:
        count = lax.axis_size(axis)
        forward = [(i, i + 1) for i in range(count - 1)]
        backward = [(target, source) for source, target in forward]
        low = lax.ppermute(
            lax.slice_in_dim(block, block.shape[dim] - width, None, axis=dim), axis, forward
        )
        high = lax.ppermute(lax.slice_in_dim(block, 0, width, axis=dim), axis, backward)
        block = jnp.concatenate([low, block, high], axis=dim)
    return block


def spread(values):
    return values[:, None, None, None]


def silu_slope(value):
    sigma = jax.nn.sigmoid(value)
    return sigma * (1.0 + value * (1.0 - sigma))


def convolve(padded, weight):
    in_chan = padded.shape[0]
    out_chan = weight.shape[3]
    span_x = padded.shape[1] - 2
    span_y = padded.shape[2] - 2
    span_z = padded.shape[3] - 2
    total = jnp.zeros((out_chan, span_x * span_y * span_z), jnp.float32)
    for shift_x in range(3):
        for shift_y in range(3):
            pieces = [
                padded[
                    :,
                    shift_x : shift_x + span_x,
                    shift_y : shift_y + span_y,
                    shift_z : shift_z + span_z,
                ]
                for shift_z in range(3)
            ]
            stacked = jnp.concatenate(pieces, axis=0).reshape(3 * in_chan, -1)
            matrix = weight[shift_x, shift_y].transpose(1, 0, 2).reshape(out_chan, 3 * in_chan)
            total = total + jnp.dot(matrix, stacked, preferred_element_type=jnp.float32)
    return total.reshape(out_chan, span_x, span_y, span_z)


def kernel_grad(padded, upstream):
    in_chan = padded.shape[0]
    out_chan = upstream.shape[0]
    span_x, span_y, span_z = (upstream.shape[1], upstream.shape[2], upstream.shape[3])
    flat = upstream.reshape(out_chan, -1)
    rows = []
    for shift_x in range(3):
        for shift_y in range(3):
            pieces = [
                padded[
                    :,
                    shift_x : shift_x + span_x,
                    shift_y : shift_y + span_y,
                    shift_z : shift_z + span_z,
                ]
                for shift_z in range(3)
            ]
            stacked = jnp.concatenate(pieces, axis=0).reshape(3 * in_chan, -1)
            product = lax.dot_general(
                flat, stacked, (((1,), (1,)), ((), ())), preferred_element_type=jnp.float32
            )
            rows.append(product.reshape(out_chan, 3, in_chan).transpose(1, 0, 2))
    return jnp.stack(rows).reshape(3, 3, 3, out_chan, in_chan)


def flipped(weight):
    return jnp.flip(weight, (0, 1, 2)).transpose(0, 1, 2, 4, 3)


def statistics(blocks, voxels):
    local_sums = jnp.stack([jnp.sum(block, axis=(1, 2, 3)) for block in blocks])
    local_squares = jnp.stack([jnp.sum(jnp.square(block), axis=(1, 2, 3)) for block in blocks])
    sums, squares = lax.psum((local_sums, local_squares), ("gx", "gy", "gz"))
    means = sums / voxels
    variance = squares / voxels - means * means
    return (means, lax.rsqrt(variance + EPSILON))


def normalize(block, means, scales, gain, bias):
    normed = (block - spread(means)) * spread(scales)
    return (normed, spread(gain) * normed + spread(bias))


def backward_layer(upstream, preact, normed, scales, gain, voxels):
    slope = upstream * silu_slope(preact)
    sum_d, sum_dx = lax.psum(
        (jnp.sum(slope, axis=(1, 2, 3)), jnp.sum(slope * normed, axis=(1, 2, 3))),
        ("gx", "gy", "gz"),
    )
    delta = spread(gain * scales) * (
        slope - spread(sum_d / voxels) - normed * spread(sum_dx / voxels)
    )
    return (delta.astype(jnp.bfloat16), sum_d, sum_dx)


def body(x_a, x_b, w_first, w_second, gain_first, bias_first, gain_second, bias_second, grad_out):
    rows_x, rows_y, rows_z = (x_a.shape[1], x_a.shape[2], x_a.shape[3])
    voxels = float(
        rows_x * rows_y * rows_z * lax.axis_size("gx") * lax.axis_size("gy") * lax.axis_size("gz")
    )
    factor = 1.0 / math.sqrt(voxels)
    volumes = jnp.stack([x_a, x_b])
    padded = extended(volumes, (("gx", 2), ("gy", 3), ("gz", 4)), 1)
    first = [convolve(padded[member], w_first) for member in range(2)]
    means, scales = statistics(first, voxels)
    hidden = []
    for member in range(2):
        normed, preact = normalize(
            first[member], means[member], scales[member], gain_first, bias_first
        )
        hidden.append((preact * jax.nn.sigmoid(preact)).astype(jnp.bfloat16))
    hidden_all = extended(jnp.stack(hidden), (("gx", 2), ("gy", 3), ("gz", 4)), 1)
    hidden_pads = [hidden_all[0], hidden_all[1]]
    input_pad_b = padded[1]
    scale_one = scales[1]
    second = [convolve(hidden_pads[member], w_second) for member in range(2)]
    means_two, scales_two = statistics(second, voxels)
    normed_a, preact_a = normalize(second[0], means_two[0], scales_two[0], gain_second, bias_second)
    y_a = (preact_a * jax.nn.sigmoid(preact_a)).astype(jnp.bfloat16)
    norm_two, pre_two = normalize(second[1], means_two[1], scales_two[1], gain_second, bias_second)
    delta_two, sum_d2, sum_x2 = backward_layer(
        grad_out.astype(jnp.float32), pre_two, norm_two, scales_two[1], gain_second, voxels
    )
    local_second = kernel_grad(hidden_pads[1], delta_two) * factor
    grad_w_second = lax.psum(local_second, ("gx", "gy", "gz"))
    delta_pad_two = extended(delta_two, (("gx", 1), ("gy", 2), ("gz", 3)), 1)
    upstream_one = convolve(delta_pad_two, flipped(w_second))
    delta_one, sum_d1, sum_x1 = backward_layer(
        upstream_one, preact, normed, scale_one, gain_first, voxels
    )
    local_first = kernel_grad(input_pad_b, delta_one) * factor
    delta_pad_one = extended(delta_one, (("gx", 1), ("gy", 2), ("gz", 3)), 1)
    dx_b = convolve(delta_pad_one, flipped(w_first)).astype(jnp.bfloat16)
    grad_w_first = lax.psum(local_first, ("gx", "gy", "gz"))
    grad_norm = jnp.stack([sum_x1, sum_d1, sum_x2, sum_d2]) * factor
    return (y_a, dx_b, grad_w_first, grad_w_second, grad_norm)


def solution(mesh):
    placed = (
        P(None, "gx", "gy", "gz"),
        P(None, "gx", "gy", "gz"),
        P(),
        P(),
        P(),
        P(),
        P(),
        P(),
        P(None, "gx", "gy", "gz"),
    )
    return jax.shard_map(
        body,
        mesh=mesh,
        in_specs=placed,
        out_specs=(P(None, "gx", "gy", "gz"), P(None, "gx", "gy", "gz"), P(), P(), P()),
        check_vma=False,
    )
```

profile of v0, /device:TPU:0, one launch (start us, length us, event | category | flops | bytes accessed | tf_op | source)
XLA Modules:
  0.0 585.4 jit_solution(11531565275628670312)
XLA Ops:
  8.4 5.0 collective-permute-start
  15.6 3.3 collective-permute-done
  18.9 4.1 collective-permute-done.1
  23.2 3.7 copy.460
  31.5 3.1 collective-permute-done.3
  34.6 6.2 %pad_maximum_fusion = bf16[2,32,4,18,128]{1,2,4,3,0:T(4,128)(2,1)S(1)} fusion(bf16[2,32,4,1,128]{1,2,4,3,0:T(4,128)(2,1)S(1)} %collective-permute-done.3, bf16[2,32,4,16,128]{1,2,4,3,0:T(4,128)(2,1)} %copy.460, bf16[2,32,4,1,128]{1,2,4,3,0:T(4,128)(2,1)S(1)} %collective-permute-done.2), kind=kLoop, calls=%fused_computation | loop fusion | flops 1179648 | bytes 2359296 | tf_op jit(solution)/shard_map/concatenate | solution.py:19
  40.8 2.1 copy-done
  43.0 4.0 collective-permute-start.4
  54.2 6.3 %copy.464 = bf16[2,32,4,18,128]{4,1,3,2,0:T(8,128)(2,1)S(1)} copy(bf16[2,32,4,18,128]{1,2,4,3,0:T(4,128)(2,1)} %copy-done) | data formatting | bytes 2359296 | tf_op jit(solution)/shard_map/concatenate | solution.py:19
  61.5 1.7 copy.463
  66.0 1.7 fusion.176
  67.7 3.2 fusion.175
  82.2 1.6 pad_maximum_fusion.19
  94.8 44.5 %all-reduce.3 = (f32[2,32]{1,0:T(2,128)S(1)}, f32[2,32]{1,0:T(2,128)S(1)}) all-reduce(f32[2,32]{1,0:T(2,128)S(1)} %pad_maximum_fusion.75, f32[2,32]{1,0:T(2,128)S(1)} %pad_maximum_fusion.74), channel_id=1, replica_groups=mesh['gx'=4,'gy'=4,'gz'=2] {'gx','gy','gz'}, use_global_device_ids=true, to_apply=%region_5.0 | all-reduce | flops 128 | bytes 1024 | tf_op jit(solution)/shard_map/psum | solution.py:88
  141.6 2.2 collective-permute-start.6
  145.9 2.7 collective-permute-done.6
  148.5 4.1 collective-permute-done.7
  153.8 5.6 copy.493
  159.4 2.1 fusion.165
  169.8 6.3 %pad_maximum_fusion.1 = bf16[2,32,4,18,128]{1,2,4,3,0:T(4,128)(2,1)S(1)} fusion(bf16[2,32,4,1,128]{1,2,4,3,0:T(4,128)(2,1)} %collective-permute-done.9, bf16[2,32,4,16,128]{1,2,4,3,0:T(4,128)(2,1)} %copy.493, bf16[2,32,4,1,128]{1,2,4,3,0:T(4,128)(2,1)S(1)} %collective-permute-done.8), kind=kLoop, calls=%fused_computation.1 | loop fusion | flops 1179648 | bytes 2359296 | tf_op jit(solution)/shard_map/concatenate | solution.py:19
  176.1 2.1 copy-done.1
  178.3 3.6 collective-permute-start.10
  185.6 2.2 dot_general.394
  195.3 7.1 %copy.497 = bf16[2,32,4,18,128]{4,1,3,2,0:T(8,128)(2,1)} copy(bf16[2,32,4,18,128]{1,2,4,3,0:T(4,128)(2,1)} %copy-done.1) | data formatting | bytes 2359296 | tf_op jit(solution)/shard_map/concatenate | solution.py:19
  204.4 2.6 pad_maximum_fusion.3
  207.2 1.8 fusion.174
  209.0 3.1 fusion.173
  213.3 3.0 fusion.171
  243.7 2.2 dot_general.408
  249.7 2.2 dot_general.404
  257.3 44.2 %all-reduce.2 = (f32[2,32]{1,0:T(2,128)S(1)}, f32[2,32]{1,0:T(2,128)S(1)}) all-reduce(f32[2,32]{1,0:T(2,128)S(1)} %pad_maximum_fusion.77, f32[2,32]{1,0:T(2,128)S(1)} %pad_maximum_fusion.76), channel_id=1, replica_groups=mesh['gx'=4,'gy'=4,'gz'=2] {'gx','gy','gz'}, use_global_device_ids=true, to_apply=%region_11.0 | all-reduce | flops 128 | bytes 1024 | tf_op jit(solution)/shard_map/psum | solution.py:88
  301.7 1.9 fusion.162
  303.6 38.6 %all-reduce.1 = (f32[32]{0:T(128)S(1)}, f32[32]{0:T(128)S(1)}) all-reduce(f32[32]{0:T(128)S(1)} %get-tuple-element.28, f32[32]{0:T(128)S(1)} %get-tuple-element.27), channel_id=1, replica_groups=mesh['gx'=4,'gy'=4,'gz'=2] {'gx','gy','gz'}, use_global_device_ids=true, to_apply=%region_15.0 | all-reduce | flops 64 | bytes 512 | tf_op jit(solution)/shard_map/psum | solution.py:101
  342.1 1.4 multiply_convert_fusion.1
  345.7 3.7 collective-permute-start.12
  349.4 1.4 collective-permute-start.13
  350.9 1.7 fusion.10
  361.8 2.7 collective-permute-done.15
  368.1 5.1 collective-permute-start.16
  376.8 2.2 maximum_maximum_fusion
  387.8 43.2 %all-reduce = (f32[32]{0:T(128)S(1)}, f32[32]{0:T(128)S(1)}) all-reduce(f32[32]{0:T(128)S(1)} %get-tuple-element.26, f32[32]{0:T(128)S(1)} %get-tuple-element.25), channel_id=1, replica_groups=mesh['gx'=4,'gy'=4,'gz'=2] {'gx','gy','gz'}, use_global_device_ids=true, to_apply=%region_19.20 | all-reduce | flops 64 | bytes 512 | tf_op jit(solution)/shard_map/psum | solution.py:101
  432.1 2.1 collective-permute-start.18
  434.2 1.6 collective-permute-start.19
  445.5 3.7 collective-permute-done.21
  452.2 4.5 collective-permute-start.22
  469.4 105.3 %all-reduce.7.cloned.1.call-done = (f32[3,3,3,32,32]{4,3,2,1,0:T(8,128)}, f32[3,3,3,32,32]{4,3,2,1,0:T(8,128)}) async-done(((f32[3,3,3,32,32]{4,3,2,1,0:T(8,128)}, f32[3,3,3,32,32]{4,3,2,1,0:T(8,128)}), (f32[3,3,3,32,32]{4,3,2,1,0:T(8,128)}, f32[3,3,3,32,32]{4,3,2,1,0:T(8,128)})) %all-reduce.7.cloned.1.call-update) | async-done | bytes 221200 | tf_op jit(solution)/shard_map/psum | solution.py:149
  574.7 1.8 copy.917
  576.5 1.8 copy.918
  (639 shorter events, 157.3 us)
Async XLA Ops:
  7.2 15.9 %copy-start.99 = (bf16[32,2,16,128]{3,2,1,0:T(8,128)(2,1)S(1)}, bf16[32,2,16,128]{3,2,1,0:T(8,128)(2,1)}, u32[]{:S(2)}) copy-start(bf16[32,2,16,128]{3,2,1,0:T(8,128)(2,1)} %param.10) | copy-start | bytes 786436
  7.2 15.9 %copy-start.98 = (bf16[32,2,16,128]{3,2,1,0:T(8,128)(2,1)S(1)}, bf16[32,2,16,128]{3,2,1,0:T(8,128)(2,1)}, u32[]{:S(2)}) copy-start(bf16[32,2,16,128]{3,2,1,0:T(8,128)(2,1)} %param.9) | copy-start | bytes 786436
  7.2 567.6 %all-reduce.7.cloned.1.call-start = ((), (), s32[]{:S(2)}) async-start(), calls=%async_computation | async-start | bytes 1769472 | tf_op jit(solution)/shard_map/psum | solution.py:149
  8.4 10.5 %collective-permute-start = (bf16[2,32,1,16,128]{4,3,2,1,0:T(8,128)(2,1)S(1)}, bf16[2,32,1,16,128]{4,3,2,1,0:T(8,128)(2,1)S(1)}, u32[]{:S(2)}, u32[]{:S(2)}) collective-permute-start(bf16[2,32,1,16,128]{4,3,2,1,0:T(8,128)(2,1)S(1)} %get-tuple-element.227), channel_id=1, source_target_pairs={{0,8},{8,16},{16,24},{1,9},{9,17},{17,25},{2,10},{10,18},{18,26},{... | collective-permute-start | bytes 786440 | tf_op jit(solution)/shard_map/ppermute | solution.py:15
  13.4 9.7 %collective-permute-start.1 = (bf16[2,32,1,16,128]{4,3,2,1,0:T(8,128)(2,1)S(1)}, bf16[2,32,1,16,128]{4,3,2,1,0:T(8,128)(2,1)S(1)}, u32[]{:S(2)}, u32[]{:S(2)}) collective-permute-start(bf16[2,32,1,16,128]{4,3,2,1,0:T(8,128)(2,1)S(1)} %get-tuple-element.228), channel_id=1, source_target_pairs={{8,0},{16,8},{24,16},{9,1},{17,9},{25,17},{10,2},{18,10},{26,18},{... | collective-permute-start | bytes 786440 | tf_op jit(solution)/shard_map/ppermute | solution.py:18
  28.2 3.3 collective-permute-start.2
  29.5 5.1 collective-permute-start.3
  31.5 16.8 %copy-start.100 = (bf16[3,3,3,32,32]{4,3,2,1,0:T(8,128)(2,1)S(1)}, bf16[3,3,3,32,32]{4,3,2,1,0:T(8,128)(2,1)}, u32[]{:S(2)}) copy-start(bf16[3,3,3,32,32]{4,3,2,1,0:T(8,128)(2,1)} %param.11) | copy-start | bytes 165892
  43.0 18.5 %collective-permute-start.4 = (bf16[2,32,4,18,1]{1,2,4,3,0:T(4,128)(2,1)S(1)}, bf16[2,32,4,18,1]{1,2,4,3,0:T(4,128)(2,1)}, u32[]{:S(2)}, u32[]{:S(2)}) collective-permute-start(bf16[2,32,4,18,1]{1,2,4,3,0:T(4,128)(2,1)S(1)} %get-tuple-element.43), channel_id=1, source_target_pairs={{0,1},{2,3},{4,5},{6,7},{8,9},{10,11},{12,13},{14,15},{16,17},{18,... | collective-permute-start | bytes 27656 | tf_op jit(solution)/shard_map/ppermute | solution.py:15
  47.0 13.5 %collective-permute-start.5 = (bf16[2,32,4,18,1]{1,2,4,3,0:T(4,128)(2,1)S(1)}, bf16[2,32,4,18,1]{1,2,4,3,0:T(4,128)(2,1)S(1)}, u32[]{:S(2)}, u32[]{:S(2)}) collective-permute-start(bf16[2,32,4,18,1]{1,2,4,3,0:T(4,128)(2,1)S(1)} %get-tuple-element.44), channel_id=1, source_target_pairs={{1,0},{3,2},{5,4},{7,6},{9,8},{11,10},{13,12},{15,14},{17,16},{19,... | collective-permute-start | bytes 27656 | tf_op jit(solution)/shard_map/ppermute | solution.py:18
  82.2 58.9 %copy-start.21 = (f32[4,8,32,128]{3,2,1,0:T(8,128)}, f32[4,8,32,128]{3,2,1,0:T(8,128)S(1)}, u32[]{:S(2)}) copy-start(f32[4,8,32,128]{3,2,1,0:T(8,128)S(1)} %copy.596) | copy-start | bytes 1572868
  92.2 48.9 %copy-start.147 = (f32[32]{0:T(128)S(1)}, f32[32]{0:T(128)}, u32[]{:S(2)}) copy-start(f32[32]{0:T(128)} %param.14) | copy-start | bytes 388
  92.2 48.9 %copy-start.149 = (f32[32]{0:T(128)S(1)}, f32[32]{0:T(128)}, u32[]{:S(2)}) copy-start(f32[32]{0:T(128)} %param.13) | copy-start | bytes 388
  141.6 6.9 %collective-permute-start.6 = (bf16[2,32,1,16,128]{4,3,2,1,0:T(8,128)(2,1)S(1)}, bf16[2,32,1,16,128]{4,3,2,1,0:T(8,128)(2,1)S(1)}, u32[]{:S(2)}, u32[]{:S(2)}) collective-permute-start(bf16[2,32,1,16,128]{4,3,2,1,0:T(8,128)(2,1)S(1)} %get-tuple-element.225), channel_id=1, source_target_pairs={{0,8},{8,16},{16,24},{1,9},{9,17},{17,25},{2,10},{10,18},{18,26},{... | collective-permute-start | bytes 786440 | tf_op jit(solution)/shard_map/ppermute | solution.py:15
  143.8 8.8 %collective-permute-start.7 = (bf16[2,32,1,16,128]{4,3,2,1,0:T(8,128)(2,1)S(1)}, bf16[2,32,1,16,128]{4,3,2,1,0:T(8,128)(2,1)S(1)}, u32[]{:S(2)}, u32[]{:S(2)}) collective-permute-start(bf16[2,32,1,16,128]{4,3,2,1,0:T(8,128)(2,1)S(1)} %get-tuple-element.226), channel_id=1, source_target_pairs={{8,0},{16,8},{24,16},{9,1},{17,9},{25,17},{10,2},{18,10},{26,18},{... | collective-permute-start | bytes 786440 | tf_op jit(solution)/shard_map/ppermute | solution.py:18
  159.4 9.7 %copy-start.126 = (bf16[32,3,32]{2,0,1:T(8,128)(2,1)S(1)}, bf16[32,3,32]{2,0,1:T(8,128)(2,1)}, u32[]{:S(2)}) copy-start(bf16[32,3,32]{2,0,1:T(8,128)(2,1)} %get-tuple-element.260) | copy-start | bytes 18436
  159.4 9.8 %copy-start.125 = (bf16[32,3,32]{2,0,1:T(8,128)(2,1)S(1)}, bf16[32,3,32]{2,0,1:T(8,128)(2,1)}, u32[]{:S(2)}) copy-start(bf16[32,3,32]{2,0,1:T(8,128)(2,1)} %get-tuple-element.261) | copy-start | bytes 18436
  159.4 9.9 %copy-start.124 = (bf16[32,3,32]{2,0,1:T(8,128)(2,1)S(1)}, bf16[32,3,32]{2,0,1:T(8,128)(2,1)}, u32[]{:S(2)}) copy-start(bf16[32,3,32]{2,0,1:T(8,128)(2,1)} %get-tuple-element.262) | copy-start | bytes 18436
  159.4 10.1 %copy-start.123 = (bf16[32,3,32]{2,0,1:T(8,128)(2,1)S(1)}, bf16[32,3,32]{2,0,1:T(8,128)(2,1)}, u32[]{:S(2)}) copy-start(bf16[32,3,32]{2,0,1:T(8,128)(2,1)} %get-tuple-element.263) | copy-start | bytes 18436
  159.4 10.2 %copy-start.122 = (bf16[32,3,32]{2,0,1:T(8,128)(2,1)S(1)}, bf16[32,3,32]{2,0,1:T(8,128)(2,1)}, u32[]{:S(2)}) copy-start(bf16[32,3,32]{2,0,1:T(8,128)(2,1)} %get-tuple-element.264) | copy-start | bytes 18436
  159.4 10.3 %copy-start.121 = (bf16[32,3,32]{2,0,1:T(8,128)(2,1)S(1)}, bf16[32,3,32]{2,0,1:T(8,128)(2,1)}, u32[]{:S(2)}) copy-start(bf16[32,3,32]{2,0,1:T(8,128)(2,1)} %get-tuple-element.265) | copy-start | bytes 18436
  161.5 8.3 %collective-permute-start.8 = (bf16[2,32,4,1,128]{1,2,4,3,0:T(4,128)(2,1)}, bf16[2,32,4,1,128]{1,2,4,3,0:T(4,128)(2,1)S(1)}, u32[]{:S(2)}, u32[]{:S(2)}) collective-permute-start(bf16[2,32,4,1,128]{1,2,4,3,0:T(4,128)(2,1)} %get-tuple-element.45), channel_id=1, source_target_pairs={{0,2},{2,4},{4,6},{1,3},{3,5},{5,7},{8,10},{10,12},{12,14},{9,11},... | collective-permute-start | bytes 196616 | tf_op jit(solution)/shard_map/ppermute | solution.py:15
  162.8 7.0 %collective-permute-start.9 = (bf16[2,32,4,1,128]{1,2,4,3,0:T(4,128)(2,1)}, bf16[2,32,4,1,128]{1,2,4,3,0:T(4,128)(2,1)}, u32[]{:S(2)}, u32[]{:S(2)}) collective-permute-start(bf16[2,32,4,1,128]{1,2,4,3,0:T(4,128)(2,1)} %get-tuple-element.46), channel_id=1, source_target_pairs={{2,0},{4,2},{6,4},{3,1},{5,3},{7,5},{10,8},{12,10},{14,12},{11,9},... | collective-permute-start | bytes 196616 | tf_op jit(solution)/shard_map/ppermute | solution.py:18
  169.8 13.4 %copy-start.146 = (f32[2,32]{1,0:T(2,128)S(1)}, f32[2,32]{1,0:T(2,128)}, u32[]{:S(2)}) copy-start(f32[2,32]{1,0:T(2,128)} %copy-done.145) | copy-start | bytes 772
  169.8 13.4 %copy-start.150 = (f32[32]{0:T(128)S(1)}, f32[32]{0:T(128)}, u32[]{:S(2)}) copy-start(f32[32]{0:T(128)} %param.13) | copy-start | bytes 388
  178.3 25.1 %collective-permute-start.10 = (bf16[2,32,4,18,1]{1,2,4,3,0:T(4,128)(2,1)S(1)}, bf16[2,32,4,18,1]{1,2,4,3,0:T(4,128)(2,1)S(1)}, u32[]{:S(2)}, u32[]{:S(2)}) collective-permute-start(bf16[2,32,4,18,1]{1,2,4,3,0:T(4,128)(2,1)S(1)} %get-tuple-element.41), channel_id=1, source_target_pairs={{0,1},{2,3},{4,5},{6,7},{8,9},{10,11},{12,13},{14,15},{16,17},{18,... | collective-permute-start | bytes 27656 | tf_op jit(solution)/shard_map/ppermute | solution.py:15
  181.9 20.5 %collective-permute-start.11 = (bf16[2,32,4,18,1]{1,2,4,3,0:T(4,128)(2,1)S(1)}, bf16[2,32,4,18,1]{1,2,4,3,0:T(4,128)(2,1)S(1)}, u32[]{:S(2)}, u32[]{:S(2)}) collective-permute-start(bf16[2,32,4,18,1]{1,2,4,3,0:T(4,128)(2,1)S(1)} %get-tuple-element.42), channel_id=1, source_target_pairs={{1,0},{3,2},{5,4},{7,6},{9,8},{11,10},{13,12},{15,14},{17,16},{19,... | collective-permute-start | bytes 27656 | tf_op jit(solution)/shard_map/ppermute | solution.py:18
  256.6 44.9 %copy-start.152 = (f32[32]{0:T(128)S(1)}, f32[32]{0:T(128)}, u32[]{:S(2)}) copy-start(f32[32]{0:T(128)} %param.15) | copy-start | bytes 388
  256.6 45.1 %copy-start.106 = (bf16[32,2,16,128]{3,2,1,0:T(8,128)(2,1)S(1)}, bf16[32,2,16,128]{3,2,1,0:T(8,128)(2,1)}, u32[]{:S(2)}) copy-start(bf16[32,2,16,128]{3,2,1,0:T(8,128)(2,1)} %param.17) | copy-start | bytes 786436
  256.6 45.1 %copy-start.151 = (f32[32]{0:T(128)S(1)}, f32[32]{0:T(128)}, u32[]{:S(2)}) copy-start(f32[32]{0:T(128)} %param.16) | copy-start | bytes 388
  257.2 44.5 %copy-start.43 = (f32[4,8,32,128]{3,2,1,0:T(8,128)S(1)}, f32[4,8,32,128]{3,2,1,0:T(8,128)}, u32[]{:S(2)}) copy-start(f32[4,8,32,128]{3,2,1,0:T(8,128)} %copy.606) | copy-start | bytes 1572868
  344.3 8.3 %copy-start.33 = (bf16[3,32,4096]{2,1,0:T(8,128)(2,1)S(1)}, bf16[3,32,4096]{2,1,0:T(8,128)(2,1)}, u32[]{:S(2)}) copy-start(bf16[3,32,4096]{2,1,0:T(8,128)(2,1)} %dot_general.398) | copy-start | bytes 2359300
  345.5 7.7 %copy-start.36 = (bf16[3,32,4096]{2,1,0:T(8,128)(2,1)S(1)}, bf16[3,32,4096]{2,1,0:T(8,128)(2,1)}, u32[]{:S(2)}) copy-start(bf16[3,32,4096]{2,1,0:T(8,128)(2,1)} %dot_general.400) | copy-start | bytes 2359300
  345.7 11.9 %collective-permute-start.12 = (bf16[32,1,16,128]{3,0,2,1:T(8,128)(2,1)}, bf16[32,1,16,128]{3,0,2,1:T(8,128)(2,1)S(1)}, u32[]{:S(2)}, u32[]{:S(2)}) collective-permute-start(bf16[32,1,16,128]{3,0,2,1:T(8,128)(2,1)} %get-tuple-element.237), channel_id=1, source_target_pairs={{0,8},{8,16},{16,24},{1,9},{9,17},{17,25},{2,10},{10,18},{18,26},{... | collective-permute-start | bytes 393224 | tf_op jit(solution)/shard_map/ppermute | solution.py:15
  349.4 8.2 %collective-permute-start.13 = (bf16[32,1,16,128]{3,0,2,1:T(8,128)(2,1)S(1)}, bf16[32,1,16,128]{3,0,2,1:T(8,128)(2,1)S(1)}, u32[]{:S(2)}, u32[]{:S(2)}) collective-permute-start(bf16[32,1,16,128]{3,0,2,1:T(8,128)(2,1)S(1)} %get-tuple-element.238), channel_id=1, source_target_pairs={{8,0},{16,8},{24,16},{9,1},{17,9},{25,17},{10,2},{18,10},{26,18},{... | collective-permute-start | bytes 393224 | tf_op jit(solution)/shard_map/ppermute | solution.py:18
  357.6 4.2 collective-permute-start.14
  358.9 5.6 collective-permute-start.15
  361.8 11.4 %copy-start.104 = (bf16[32,4,1,128]{3,0,2,1:T(8,128)(2,1)}, bf16[32,4,1,128]{3,0,2,1:T(8,128)(2,1)S(1)}, u32[]{:S(2)}) copy-start(bf16[32,4,1,128]{3,0,2,1:T(8,128)(2,1)S(1)} %collective-permute-done.14) | copy-start | bytes 98308
  364.5 8.7 %copy-start.105 = (bf16[32,4,1,128]{3,0,2,1:T(8,128)(2,1)}, bf16[32,4,1,128]{3,0,2,1:T(8,128)(2,1)S(1)}, u32[]{:S(2)}) copy-start(bf16[32,4,1,128]{3,0,2,1:T(8,128)(2,1)S(1)} %collective-permute-done.15) | copy-start | bytes 98308
  366.8 8.7 %collective-permute-start.17 = (bf16[32,4,18,1]{0,2,3,1:T(8,128)(2,1)S(1)}, bf16[32,4,18,1]{0,2,3,1:T(8,128)(2,1)}, u32[]{:S(2)}, u32[]{:S(2)}) collective-permute-start(bf16[32,4,18,1]{0,2,3,1:T(8,128)(2,1)S(1)} %copy.531), channel_id=1, source_target_pairs={{1,0},{3,2},{5,4},{7,6},{9,8},{11,10},{13,12},{15,14},{17,16},{19,... | collective-permute-start | bytes 13832 | tf_op jit(solution)/shard_map/ppermute | solution.py:18
  368.1 6.8 %collective-permute-start.16 = (bf16[32,4,18,1]{0,2,3,1:T(8,128)(2,1)}, bf16[32,4,18,1]{0,2,3,1:T(8,128)(2,1)S(1)}, u32[]{:S(2)}, u32[]{:S(2)}) collective-permute-start(bf16[32,4,18,1]{0,2,3,1:T(8,128)(2,1)} %copy.529), channel_id=1, source_target_pairs={{0,1},{2,3},{4,5},{6,7},{8,9},{10,11},{12,13},{14,15},{16,17},{18,... | collective-permute-start | bytes 13832 | tf_op jit(solution)/shard_map/ppermute | solution.py:15
  387.8 43.5 %copy-start.22 = (f32[4,8,32,128]{3,2,1,0:T(8,128)S(1)}, f32[4,8,32,128]{3,2,1,0:T(8,128)}, u32[]{:S(2)}) copy-start(f32[4,8,32,128]{3,2,1,0:T(8,128)} %copy-done.21) | copy-start | bytes 1572868
  432.1 10.2 %collective-permute-start.18 = (bf16[32,1,16,128]{3,0,2,1:T(8,128)(2,1)S(1)}, bf16[32,1,16,128]{3,0,2,1:T(8,128)(2,1)S(1)}, u32[]{:S(2)}, u32[]{:S(2)}) collective-permute-start(bf16[32,1,16,128]{3,0,2,1:T(8,128)(2,1)S(1)} %get-tuple-element.232), channel_id=1, source_target_pairs={{0,8},{8,16},{16,24},{1,9},{9,17},{17,25},{2,10},{10,18},{18,26},{... | collective-permute-start | bytes 393224 | tf_op jit(solution)/shard_map/ppermute | solution.py:15
  434.2 8.1 %collective-permute-start.19 = (bf16[32,1,16,128]{3,0,2,1:T(8,128)(2,1)S(1)}, bf16[32,1,16,128]{3,0,2,1:T(8,128)(2,1)S(1)}, u32[]{:S(2)}, u32[]{:S(2)}) collective-permute-start(bf16[32,1,16,128]{3,0,2,1:T(8,128)(2,1)S(1)} %get-tuple-element.233), channel_id=1, source_target_pairs={{8,0},{16,8},{24,16},{9,1},{17,9},{25,17},{10,2},{18,10},{26,18},{... | collective-permute-start | bytes 393224 | tf_op jit(solution)/shard_map/ppermute | solution.py:18
  442.3 3.2 collective-permute-start.20
  443.6 5.6 collective-permute-start.21
  450.9 7.9 %collective-permute-start.23 = (bf16[32,4,18,1]{0,2,3,1:T(8,128)(2,1)S(1)}, bf16[32,4,18,1]{0,2,3,1:T(8,128)(2,1)S(1)}, u32[]{:S(2)}, u32[]{:S(2)}) collective-permute-start(bf16[32,4,18,1]{0,2,3,1:T(8,128)(2,1)S(1)} %copy.546), channel_id=1, source_target_pairs={{1,0},{3,2},{5,4},{7,6},{9,8},{11,10},{13,12},{15,14},{17,16},{19,... | collective-permute-start | bytes 13832 | tf_op jit(solution)/shard_map/ppermute | solution.py:18
  452.2 6.1 %collective-permute-start.22 = (bf16[32,4,18,1]{0,2,3,1:T(8,128)(2,1)S(1)}, bf16[32,4,18,1]{0,2,3,1:T(8,128)(2,1)S(1)}, u32[]{:S(2)}, u32[]{:S(2)}) collective-permute-start(bf16[32,4,18,1]{0,2,3,1:T(8,128)(2,1)S(1)} %copy.544), channel_id=1, source_target_pairs={{0,1},{2,3},{4,5},{6,7},{8,9},{10,11},{12,13},{14,15},{16,17},{18,... | collective-permute-start | bytes 13832 | tf_op jit(solution)/shard_map/ppermute | solution.py:15
  (130 other events, 218.3 us)
Sparse Core Ops, SparseCore 0:
  442.4 132.2 all-reduce.6
where the time goes:
time: 592 us; the launch traced here: 585 us
  blocking collectives  170 us (29%)
  local copies, waits for them, and re-layouts  139 us (23%)
  waiting for transfers between devices  131 us (22%)
  starting transfers between devices  51.5 us (9%)
  other arithmetic  40.1 us (7%)
  matrix products  36.3 us (6%)
  between operations  17.5 us (3%)
    psum x1, waiting for transfers between devices, body(): grad_w_first = lax.psum(local_first, ('gx', 'gy', 'gz'))  105 us
    psum x2, blocking collectives, statistics(): sums, squares = lax.psum((local_sums, local_squares), ('gx', 'gy', 'gz'))  88.7 us
    psum x2, blocking collectives, backward_layer(): lax.psum((jnp.sum(slope, axis=(1, 2, 3)), jnp.sum(slope * normed, axis=(1...  81.7 us
    ppermute x12, starting transfers between devices, extended(): lax.ppermute(lax.slice_in_dim(block, block.shape[dim] - width, None, axis...  35.5 us
    dot_general x18, local copies, waits for them, and re-layouts, kernel_grad(): lax.dot_general(flat, stacked, (((1,), (1,)), ((), ())), preferred_elemen...  25 us
    dot_general x54, matrix products, convolve(): total = total + jnp.dot(matrix, stacked, preferred_element_type=jnp.float32)  24.8 us
    unnamed x315, local copies, waits for them, and re-layouts  23.4 us
    concatenate x4, local copies, waits for them, and re-layouts, extended(): block = jnp.concatenate([low, block, high], axis=dim)  22.8 us
  transfers between devices with their start and end apart: 25, of which 10 were waited for; matrix products, arithmetic and copies ran while one was open for 12% of the time, Pallas kernels for 0%

commit v1 on v0

--- a/solution.py
+++ b/solution.py
@@ -99,8 +99,8 @@
 def backward_layer(upstream, preact, normed, scales, gain, voxels):
     slope = upstream * silu_slope(preact)
     sum_d, sum_dx = lax.psum(
-        (jnp.sum(slope, axis=(1, 2, 3)), jnp.sum(slope * normed, axis=(1, 2, 3))),
-        ("gx", "gy", "gz"),
+        lax.psum((jnp.sum(slope, axis=(1, 2, 3)), jnp.sum(slope * normed, axis=(1, 2, 3))), "gx"),
+        ("gy", "gz"),
     )
     delta = spread(gain * scales) * (
         slope - spread(sum_d / voxels) - normed * spread(sum_dx / voxels)

time: 592 us -> 554 us (0.936)
  blocking collectives: 170 us -> 139 us
    psum x2, blocking collectives: 81.7 us -> 21.8 us  [backward_layer(): lax.psum((jnp.sum(slope, axis=(1, 2, 3)), jnp.sum(slope * normed, axis=(1...]
    psum x0 -> x2, blocking collectives: none -> 29 us  [backward_layer(): lax.psum(lax.psum((jnp.sum(slope, axis=(1, 2, 3)), jnp.sum(slope * normed...]
  transfers between devices with their start and end apart: 25 -> 25, of which waited for: 10 -> 10; matrix products, arithmetic and copies ran while one was open for 12% -> 13% of each run, Pallas kernels for 0% -> 0%
where the time goes in v1:
time: 554 us; the launch traced here: 547 us
  local copies, waits for them, and re-layouts  139 us (25%)
  blocking collectives  139 us (25%)
  waiting for transfers between devices  126 us (23%)
  starting transfers between devices  49.9 us (9%)
  other arithmetic  40.1 us (7%)
  matrix products  36.3 us (7%)
  between operations  17.5 us (3%)
    psum x1, waiting for transfers between devices, body(): grad_w_first = lax.psum(local_first, ('gx', 'gy', 'gz'))  103 us
    psum x2, blocking collectives, statistics(): sums, squares = lax.psum((local_sums, local_squares), ('gx', 'gy', 'gz'))  88.7 us
    ppermute x12, starting transfers between devices, extended(): lax.ppermute(lax.slice_in_dim(block, block.shape[dim] - width, None, axis...  33.8 us
    psum x2, blocking collectives, backward_layer(): lax.psum(lax.psum((jnp.sum(slope, axis=(1, 2, 3)), jnp.sum(slope * normed...  29 us
    dot_general x18, local copies, waits for them, and re-layouts, kernel_grad(): lax.dot_general(flat, stacked, (((1,), (1,)), ((), ())), preferred_elemen...  25 us
    dot_general x54, matrix products, convolve(): total = total + jnp.dot(matrix, stacked, preferred_element_type=jnp.float32)  24.8 us
    unnamed x315, local copies, waits for them, and re-layouts  23.4 us
    concatenate x4, local copies, waits for them, and re-layouts, extended(): block = jnp.concatenate([low, block, high], axis=dim)  22.8 us
  transfers between devices with their start and end apart: 25, of which 10 were waited for; matrix products, arithmetic and copies ran while one was open for 13% of the time, Pallas kernels for 0%

profile of v1, /device:TPU:0, one launch (start us, length us, event | category | flops | bytes accessed | tf_op | source)
XLA Modules:
  0.0 547.5 jit_solution(11806351981170898260)
XLA Ops:
  8.4 5.0 collective-permute-start
  15.6 3.3 collective-permute-done
  18.9 4.1 collective-permute-done.1
  23.2 3.7 copy.460
  31.5 3.1 collective-permute-done.3
  34.6 6.2 %pad_maximum_fusion = bf16[2,32,4,18,128]{1,2,4,3,0:T(4,128)(2,1)S(1)} fusion(bf16[2,32,4,1,128]{1,2,4,3,0:T(4,128)(2,1)S(1)} %collective-permute-done.3, bf16[2,32,4,16,128]{1,2,4,3,0:T(4,128)(2,1)} %copy.460, bf16[2,32,4,1,128]{1,2,4,3,0:T(4,128)(2,1)S(1)} %collective-permute-done.2), kind=kLoop, calls=%fused_computation | loop fusion | flops 1179648 | bytes 2359296 | tf_op jit(solution)/shard_map/concatenate | solution.py:19
  40.8 2.1 copy-done
  43.0 4.0 collective-permute-start.4
  54.2 6.3 %copy.464 = bf16[2,32,4,18,128]{4,1,3,2,0:T(8,128)(2,1)S(1)} copy(bf16[2,32,4,18,128]{1,2,4,3,0:T(4,128)(2,1)} %copy-done) | data formatting | bytes 2359296 | tf_op jit(solution)/shard_map/concatenate | solution.py:19
  61.5 1.7 copy.463
  66.0 1.7 fusion.176
  67.7 3.2 fusion.175
  82.2 1.6 pad_maximum_fusion.19
  94.8 44.5 %all-reduce.1 = (f32[2,32]{1,0:T(2,128)S(1)}, f32[2,32]{1,0:T(2,128)S(1)}) all-reduce(f32[2,32]{1,0:T(2,128)S(1)} %pad_maximum_fusion.75, f32[2,32]{1,0:T(2,128)S(1)} %pad_maximum_fusion.74), channel_id=1, replica_groups=mesh['gx'=4,'gy'=4,'gz'=2] {'gx','gy','gz'}, use_global_device_ids=true, to_apply=%region_5.0 | all-reduce | flops 128 | bytes 1024 | tf_op jit(solution)/shard_map/psum | solution.py:88
  141.6 2.2 collective-permute-start.6
  145.9 2.7 collective-permute-done.6
  148.5 4.1 collective-permute-done.7
  153.8 5.6 %copy.493 = bf16[2,32,4,16,128]{1,2,4,3,0:T(4,128)(2,1)} copy(bf16[2,32,4,16,128]{4,3,2,1,0:T(8,128)(2,1)} %pad_maximum_fusion.7) | data formatting | bytes 2097152 | tf_op jit(solution)/shard_map/concatenate | solution.py:19
  159.4 2.1 fusion.165
  169.8 6.3 %pad_maximum_fusion.1 = bf16[2,32,4,18,128]{1,2,4,3,0:T(4,128)(2,1)S(1)} fusion(bf16[2,32,4,1,128]{1,2,4,3,0:T(4,128)(2,1)} %collective-permute-done.9, bf16[2,32,4,16,128]{1,2,4,3,0:T(4,128)(2,1)} %copy.493, bf16[2,32,4,1,128]{1,2,4,3,0:T(4,128)(2,1)S(1)} %collective-permute-done.8), kind=kLoop, calls=%fused_computation.1 | loop fusion | flops 1179648 | bytes 2359296 | tf_op jit(solution)/shard_map/concatenate | solution.py:19
  176.1 2.1 copy-done.1
  178.3 3.6 collective-permute-start.10
  185.6 2.2 dot_general.394
  195.2 7.1 %copy.497 = bf16[2,32,4,18,128]{4,1,3,2,0:T(8,128)(2,1)} copy(bf16[2,32,4,18,128]{1,2,4,3,0:T(4,128)(2,1)} %copy-done.1) | data formatting | bytes 2359296 | tf_op jit(solution)/shard_map/concatenate | solution.py:19
  204.3 2.6 pad_maximum_fusion.3
  207.1 1.8 fusion.174
  208.9 3.1 fusion.173
  213.2 3.0 fusion.171
  243.6 2.2 dot_general.408
  249.6 2.2 dot_general.404
  257.3 44.2 %all-reduce = (f32[2,32]{1,0:T(2,128)S(1)}, f32[2,32]{1,0:T(2,128)S(1)}) all-reduce(f32[2,32]{1,0:T(2,128)S(1)} %pad_maximum_fusion.77, f32[2,32]{1,0:T(2,128)S(1)} %pad_maximum_fusion.76), channel_id=1, replica_groups=mesh['gx'=4,'gy'=4,'gz'=2] {'gx','gy','gz'}, use_global_device_ids=true, to_apply=%region_11.0 | all-reduce | flops 128 | bytes 1024 | tf_op jit(solution)/shard_map/psum | solution.py:88
  301.6 1.8 fusion.162
  303.5 10.6 %all-reduce.6 = (f32[32]{0:T(128)S(1)}, f32[32]{0:T(128)S(1)}) all-reduce(f32[32]{0:T(128)S(1)} %get-tuple-element.28, f32[32]{0:T(128)S(1)} %get-tuple-element.27), channel_id=1, replica_groups=mesh['gx'=4,'gy'=4,'gz'=2] {'gx'}, use_global_device_ids=true, to_apply=%region_16.0 | all-reduce | flops 64 | bytes 512 | tf_op jit(solution)/shard_map/psum | solution.py:102
  314.1 14.3 %all-reduce.4 = (f32[32]{0:T(128)S(1)}, f32[32]{0:T(128)S(1)}) all-reduce(f32[32]{0:T(128)S(1)} %get-tuple-element.41, f32[32]{0:T(128)S(1)} %get-tuple-element.42), channel_id=1, replica_groups=mesh['gx'=4,'gy'=4,'gz'=2] {'gy','gz'}, use_global_device_ids=true, to_apply=%region_17.0 | all-reduce | flops 64 | bytes 512 | tf_op jit(solution)/shard_map/psum | solution.py:101
  331.9 1.7 collective-permute-start.12
  335.1 1.7 fusion.10
  341.9 1.7 collective-permute-start.14
  350.2 5.1 collective-permute-start.16
  358.9 2.2 maximum_maximum_fusion
  370.0 11.1 %all-reduce.5 = (f32[32]{0:T(128)S(1)}, f32[32]{0:T(128)S(1)}) all-reduce(f32[32]{0:T(128)S(1)} %get-tuple-element.26, f32[32]{0:T(128)S(1)} %get-tuple-element.25), channel_id=1, replica_groups=mesh['gx'=4,'gy'=4,'gz'=2] {'gx'}, use_global_device_ids=true, to_apply=%region_22.23 | all-reduce | flops 64 | bytes 512 | tf_op jit(solution)/shard_map/psum | solution.py:102
  381.1 14.7 %all-reduce.3 = (f32[32]{0:T(128)S(1)}, f32[32]{0:T(128)S(1)}) all-reduce(f32[32]{0:T(128)S(1)} %get-tuple-element.39, f32[32]{0:T(128)S(1)} %get-tuple-element.40), channel_id=1, replica_groups=mesh['gx'=4,'gy'=4,'gz'=2] {'gy','gz'}, use_global_device_ids=true, to_apply=%region_23.24 | all-reduce | flops 64 | bytes 512 | tf_op jit(solution)/shard_map/psum | solution.py:101
  398.4 1.6 collective-permute-start.19
  406.5 1.8 collective-permute-start.20
  410.2 3.0 collective-permute-done.21
  416.1 4.5 collective-permute-start.22
  433.4 103.4 %all-reduce.9.cloned.1.call-done = (f32[3,3,3,32,32]{4,3,2,1,0:T(8,128)}, f32[3,3,3,32,32]{4,3,2,1,0:T(8,128)}) async-done(((f32[3,3,3,32,32]{4,3,2,1,0:T(8,128)}, f32[3,3,3,32,32]{4,3,2,1,0:T(8,128)}), (f32[3,3,3,32,32]{4,3,2,1,0:T(8,128)}, f32[3,3,3,32,32]{4,3,2,1,0:T(8,128)})) %all-reduce.9.cloned.1.call-update) | async-done | bytes 221200 | tf_op jit(solution)/shard_map/psum | solution.py:149
  536.8 1.8 copy.917
  538.6 1.8 copy.918
  (641 shorter events, 159.2 us)
Async XLA Ops:
  7.2 15.9 %copy-start.99 = (bf16[32,2,16,128]{3,2,1,0:T(8,128)(2,1)S(1)}, bf16[32,2,16,128]{3,2,1,0:T(8,128)(2,1)}, u32[]{:S(2)}) copy-start(bf16[32,2,16,128]{3,2,1,0:T(8,128)(2,1)} %param.10) | copy-start | bytes 786436
  7.2 15.9 %copy-start.98 = (bf16[32,2,16,128]{3,2,1,0:T(8,128)(2,1)S(1)}, bf16[32,2,16,128]{3,2,1,0:T(8,128)(2,1)}, u32[]{:S(2)}) copy-start(bf16[32,2,16,128]{3,2,1,0:T(8,128)(2,1)} %param.9) | copy-start | bytes 786436
  7.2 529.6 %all-reduce.9.cloned.1.call-start = ((), (), s32[]{:S(2)}) async-start(), calls=%async_computation | async-start | bytes 1769472 | tf_op jit(solution)/shard_map/psum | solution.py:149
  8.4 10.5 %collective-permute-start = (bf16[2,32,1,16,128]{4,3,2,1,0:T(8,128)(2,1)S(1)}, bf16[2,32,1,16,128]{4,3,2,1,0:T(8,128)(2,1)S(1)}, u32[]{:S(2)}, u32[]{:S(2)}) collective-permute-start(bf16[2,32,1,16,128]{4,3,2,1,0:T(8,128)(2,1)S(1)} %get-tuple-element.231), channel_id=1, source_target_pairs={{0,8},{8,16},{16,24},{1,9},{9,17},{17,25},{2,10},{10,18},{18,26},{... | collective-permute-start | bytes 786440 | tf_op jit(solution)/shard_map/ppermute | solution.py:15
  13.4 9.7 %collective-permute-start.1 = (bf16[2,32,1,16,128]{4,3,2,1,0:T(8,128)(2,1)S(1)}, bf16[2,32,1,16,128]{4,3,2,1,0:T(8,128)(2,1)S(1)}, u32[]{:S(2)}, u32[]{:S(2)}) collective-permute-start(bf16[2,32,1,16,128]{4,3,2,1,0:T(8,128)(2,1)S(1)} %get-tuple-element.232), channel_id=1, source_target_pairs={{8,0},{16,8},{24,16},{9,1},{17,9},{25,17},{10,2},{18,10},{26,18},{... | collective-permute-start | bytes 786440 | tf_op jit(solution)/shard_map/ppermute | solution.py:18
  23.2 7.6 %copy-start.101 = (bf16[3,3,3,32,32]{4,3,2,1,0:T(8,128)(2,1)S(1)}, bf16[3,3,3,32,32]{4,3,2,1,0:T(8,128)(2,1)}, u32[]{:S(2)}) copy-start(bf16[3,3,3,32,32]{4,3,2,1,0:T(8,128)(2,1)} %param.12) | copy-start | bytes 165892
  28.2 3.3 collective-permute-start.2
  29.5 5.1 collective-permute-start.3
  31.5 16.8 %copy-start.100 = (bf16[3,3,3,32,32]{4,3,2,1,0:T(8,128)(2,1)S(1)}, bf16[3,3,3,32,32]{4,3,2,1,0:T(8,128)(2,1)}, u32[]{:S(2)}) copy-start(bf16[3,3,3,32,32]{4,3,2,1,0:T(8,128)(2,1)} %param.11) | copy-start | bytes 165892
  43.0 18.5 %collective-permute-start.4 = (bf16[2,32,4,18,1]{1,2,4,3,0:T(4,128)(2,1)S(1)}, bf16[2,32,4,18,1]{1,2,4,3,0:T(4,128)(2,1)}, u32[]{:S(2)}, u32[]{:S(2)}) collective-permute-start(bf16[2,32,4,18,1]{1,2,4,3,0:T(4,128)(2,1)S(1)} %get-tuple-element.47), channel_id=1, source_target_pairs={{0,1},{2,3},{4,5},{6,7},{8,9},{10,11},{12,13},{14,15},{16,17},{18,... | collective-permute-start | bytes 27656 | tf_op jit(solution)/shard_map/ppermute | solution.py:15
  47.0 13.5 %collective-permute-start.5 = (bf16[2,32,4,18,1]{1,2,4,3,0:T(4,128)(2,1)S(1)}, bf16[2,32,4,18,1]{1,2,4,3,0:T(4,128)(2,1)S(1)}, u32[]{:S(2)}, u32[]{:S(2)}) collective-permute-start(bf16[2,32,4,18,1]{1,2,4,3,0:T(4,128)(2,1)S(1)} %get-tuple-element.48), channel_id=1, source_target_pairs={{1,0},{3,2},{5,4},{7,6},{9,8},{11,10},{13,12},{15,14},{17,16},{19,... | collective-permute-start | bytes 27656 | tf_op jit(solution)/shard_map/ppermute | solution.py:18
  82.2 58.9 %copy-start.21 = (f32[4,8,32,128]{3,2,1,0:T(8,128)}, f32[4,8,32,128]{3,2,1,0:T(8,128)S(1)}, u32[]{:S(2)}) copy-start(f32[4,8,32,128]{3,2,1,0:T(8,128)S(1)} %copy.596) | copy-start | bytes 1572868
  92.2 48.9 %copy-start.147 = (f32[32]{0:T(128)S(1)}, f32[32]{0:T(128)}, u32[]{:S(2)}) copy-start(f32[32]{0:T(128)} %param.14) | copy-start | bytes 388
  92.2 48.9 %copy-start.149 = (f32[32]{0:T(128)S(1)}, f32[32]{0:T(128)}, u32[]{:S(2)}) copy-start(f32[32]{0:T(128)} %param.13) | copy-start | bytes 388
  141.6 6.9 %collective-permute-start.6 = (bf16[2,32,1,16,128]{4,3,2,1,0:T(8,128)(2,1)S(1)}, bf16[2,32,1,16,128]{4,3,2,1,0:T(8,128)(2,1)S(1)}, u32[]{:S(2)}, u32[]{:S(2)}) collective-permute-start(bf16[2,32,1,16,128]{4,3,2,1,0:T(8,128)(2,1)S(1)} %get-tuple-element.229), channel_id=1, source_target_pairs={{0,8},{8,16},{16,24},{1,9},{9,17},{17,25},{2,10},{10,18},{18,26},{... | collective-permute-start | bytes 786440 | tf_op jit(solution)/shard_map/ppermute | solution.py:15
  143.8 8.8 %collective-permute-start.7 = (bf16[2,32,1,16,128]{4,3,2,1,0:T(8,128)(2,1)S(1)}, bf16[2,32,1,16,128]{4,3,2,1,0:T(8,128)(2,1)S(1)}, u32[]{:S(2)}, u32[]{:S(2)}) collective-permute-start(bf16[2,32,1,16,128]{4,3,2,1,0:T(8,128)(2,1)S(1)} %get-tuple-element.230), channel_id=1, source_target_pairs={{8,0},{16,8},{24,16},{9,1},{17,9},{25,17},{10,2},{18,10},{26,18},{... | collective-permute-start | bytes 786440 | tf_op jit(solution)/shard_map/ppermute | solution.py:18
  159.4 9.7 %copy-start.126 = (bf16[32,3,32]{2,0,1:T(8,128)(2,1)S(1)}, bf16[32,3,32]{2,0,1:T(8,128)(2,1)}, u32[]{:S(2)}) copy-start(bf16[32,3,32]{2,0,1:T(8,128)(2,1)} %get-tuple-element.264) | copy-start | bytes 18436
  159.4 9.8 %copy-start.125 = (bf16[32,3,32]{2,0,1:T(8,128)(2,1)S(1)}, bf16[32,3,32]{2,0,1:T(8,128)(2,1)}, u32[]{:S(2)}) copy-start(bf16[32,3,32]{2,0,1:T(8,128)(2,1)} %get-tuple-element.265) | copy-start | bytes 18436
  159.4 9.9 %copy-start.124 = (bf16[32,3,32]{2,0,1:T(8,128)(2,1)S(1)}, bf16[32,3,32]{2,0,1:T(8,128)(2,1)}, u32[]{:S(2)}) copy-start(bf16[32,3,32]{2,0,1:T(8,128)(2,1)} %get-tuple-element.266) | copy-start | bytes 18436
  159.4 10.0 %copy-start.123 = (bf16[32,3,32]{2,0,1:T(8,128)(2,1)S(1)}, bf16[32,3,32]{2,0,1:T(8,128)(2,1)}, u32[]{:S(2)}) copy-start(bf16[32,3,32]{2,0,1:T(8,128)(2,1)} %get-tuple-element.267) | copy-start | bytes 18436
  159.4 10.2 %copy-start.122 = (bf16[32,3,32]{2,0,1:T(8,128)(2,1)S(1)}, bf16[32,3,32]{2,0,1:T(8,128)(2,1)}, u32[]{:S(2)}) copy-start(bf16[32,3,32]{2,0,1:T(8,128)(2,1)} %get-tuple-element.268) | copy-start | bytes 18436
  159.4 10.3 %copy-start.121 = (bf16[32,3,32]{2,0,1:T(8,128)(2,1)S(1)}, bf16[32,3,32]{2,0,1:T(8,128)(2,1)}, u32[]{:S(2)}) copy-start(bf16[32,3,32]{2,0,1:T(8,128)(2,1)} %get-tuple-element.269) | copy-start | bytes 18436
  161.5 8.3 %collective-permute-start.8 = (bf16[2,32,4,1,128]{1,2,4,3,0:T(4,128)(2,1)}, bf16[2,32,4,1,128]{1,2,4,3,0:T(4,128)(2,1)S(1)}, u32[]{:S(2)}, u32[]{:S(2)}) collective-permute-start(bf16[2,32,4,1,128]{1,2,4,3,0:T(4,128)(2,1)} %get-tuple-element.49), channel_id=1, source_target_pairs={{0,2},{2,4},{4,6},{1,3},{3,5},{5,7},{8,10},{10,12},{12,14},{9,11},... | collective-permute-start | bytes 196616 | tf_op jit(solution)/shard_map/ppermute | solution.py:15
  162.8 7.0 %collective-permute-start.9 = (bf16[2,32,4,1,128]{1,2,4,3,0:T(4,128)(2,1)}, bf16[2,32,4,1,128]{1,2,4,3,0:T(4,128)(2,1)}, u32[]{:S(2)}, u32[]{:S(2)}) collective-permute-start(bf16[2,32,4,1,128]{1,2,4,3,0:T(4,128)(2,1)} %get-tuple-element.50), channel_id=1, source_target_pairs={{2,0},{4,2},{6,4},{3,1},{5,3},{7,5},{10,8},{12,10},{14,12},{11,9},... | collective-permute-start | bytes 196616 | tf_op jit(solution)/shard_map/ppermute | solution.py:18
  169.8 13.4 %copy-start.146 = (f32[2,32]{1,0:T(2,128)S(1)}, f32[2,32]{1,0:T(2,128)}, u32[]{:S(2)}) copy-start(f32[2,32]{1,0:T(2,128)} %copy-done.145) | copy-start | bytes 772
  169.8 13.4 %copy-start.150 = (f32[32]{0:T(128)S(1)}, f32[32]{0:T(128)}, u32[]{:S(2)}) copy-start(f32[32]{0:T(128)} %param.13) | copy-start | bytes 388
  178.3 25.1 %collective-permute-start.10 = (bf16[2,32,4,18,1]{1,2,4,3,0:T(4,128)(2,1)S(1)}, bf16[2,32,4,18,1]{1,2,4,3,0:T(4,128)(2,1)S(1)}, u32[]{:S(2)}, u32[]{:S(2)}) collective-permute-start(bf16[2,32,4,18,1]{1,2,4,3,0:T(4,128)(2,1)S(1)} %get-tuple-element.45), channel_id=1, source_target_pairs={{0,1},{2,3},{4,5},{6,7},{8,9},{10,11},{12,13},{14,15},{16,17},{18,... | collective-permute-start | bytes 27656 | tf_op jit(solution)/shard_map/ppermute | solution.py:15
  181.9 20.5 %collective-permute-start.11 = (bf16[2,32,4,18,1]{1,2,4,3,0:T(4,128)(2,1)S(1)}, bf16[2,32,4,18,1]{1,2,4,3,0:T(4,128)(2,1)S(1)}, u32[]{:S(2)}, u32[]{:S(2)}) collective-permute-start(bf16[2,32,4,18,1]{1,2,4,3,0:T(4,128)(2,1)S(1)} %get-tuple-element.46), channel_id=1, source_target_pairs={{1,0},{3,2},{5,4},{7,6},{9,8},{11,10},{13,12},{15,14},{17,16},{19,... | collective-permute-start | bytes 27656 | tf_op jit(solution)/shard_map/ppermute | solution.py:18
  256.5 44.9 %copy-start.152 = (f32[32]{0:T(128)S(1)}, f32[32]{0:T(128)}, u32[]{:S(2)}) copy-start(f32[32]{0:T(128)} %param.15) | copy-start | bytes 388
  256.5 45.1 %copy-start.106 = (bf16[32,2,16,128]{3,2,1,0:T(8,128)(2,1)S(1)}, bf16[32,2,16,128]{3,2,1,0:T(8,128)(2,1)}, u32[]{:S(2)}) copy-start(bf16[32,2,16,128]{3,2,1,0:T(8,128)(2,1)} %param.17) | copy-start | bytes 786436
  256.6 45.1 %copy-start.151 = (f32[32]{0:T(128)S(1)}, f32[32]{0:T(128)}, u32[]{:S(2)}) copy-start(f32[32]{0:T(128)} %param.16) | copy-start | bytes 388
  257.1 44.5 %copy-start.43 = (f32[4,8,32,128]{3,2,1,0:T(8,128)S(1)}, f32[4,8,32,128]{3,2,1,0:T(8,128)}, u32[]{:S(2)}) copy-start(f32[4,8,32,128]{3,2,1,0:T(8,128)} %copy.606) | copy-start | bytes 1572868
  330.6 6.3 %copy-start.33 = (bf16[3,32,4096]{2,1,0:T(8,128)(2,1)S(1)}, bf16[3,32,4096]{2,1,0:T(8,128)(2,1)}, u32[]{:S(2)}) copy-start(bf16[3,32,4096]{2,1,0:T(8,128)(2,1)} %dot_general.398) | copy-start | bytes 2359300
  331.9 9.9 %collective-permute-start.12 = (bf16[32,1,16,128]{3,0,2,1:T(8,128)(2,1)}, bf16[32,1,16,128]{3,0,2,1:T(8,128)(2,1)S(1)}, u32[]{:S(2)}, u32[]{:S(2)}) collective-permute-start(bf16[32,1,16,128]{3,0,2,1:T(8,128)(2,1)} %get-tuple-element.241), channel_id=1, source_target_pairs={{0,8},{8,16},{16,24},{1,9},{9,17},{17,25},{2,10},{10,18},{18,26},{... | collective-permute-start | bytes 393224 | tf_op jit(solution)/shard_map/ppermute | solution.py:15
  333.7 8.2 %collective-permute-start.13 = (bf16[32,1,16,128]{3,0,2,1:T(8,128)(2,1)S(1)}, bf16[32,1,16,128]{3,0,2,1:T(8,128)(2,1)S(1)}, u32[]{:S(2)}, u32[]{:S(2)}) collective-permute-start(bf16[32,1,16,128]{3,0,2,1:T(8,128)(2,1)S(1)} %get-tuple-element.242), channel_id=1, source_target_pairs={{8,0},{16,8},{24,16},{9,1},{17,9},{25,17},{10,2},{18,10},{26,18},{... | collective-permute-start | bytes 393224 | tf_op jit(solution)/shard_map/ppermute | solution.py:18
  341.9 4.6 collective-permute-start.14
  343.6 3.1 collective-permute-start.15
  346.5 8.9 %copy-start.104 = (bf16[32,4,1,128]{3,0,2,1:T(8,128)(2,1)}, bf16[32,4,1,128]{3,0,2,1:T(8,128)(2,1)S(1)}, u32[]{:S(2)}) copy-start(bf16[32,4,1,128]{3,0,2,1:T(8,128)(2,1)S(1)} %collective-permute-done.14) | copy-start | bytes 98308
  346.7 8.7 %copy-start.105 = (bf16[32,4,1,128]{3,0,2,1:T(8,128)(2,1)}, bf16[32,4,1,128]{3,0,2,1:T(8,128)(2,1)S(1)}, u32[]{:S(2)}) copy-start(bf16[32,4,1,128]{3,0,2,1:T(8,128)(2,1)S(1)} %collective-permute-done.15) | copy-start | bytes 98308
  348.9 8.7 %collective-permute-start.17 = (bf16[32,4,18,1]{0,2,3,1:T(8,128)(2,1)S(1)}, bf16[32,4,18,1]{0,2,3,1:T(8,128)(2,1)}, u32[]{:S(2)}, u32[]{:S(2)}) collective-permute-start(bf16[32,4,18,1]{0,2,3,1:T(8,128)(2,1)S(1)} %copy.531), channel_id=1, source_target_pairs={{1,0},{3,2},{5,4},{7,6},{9,8},{11,10},{13,12},{15,14},{17,16},{19,... | collective-permute-start | bytes 13832 | tf_op jit(solution)/shard_map/ppermute | solution.py:18
  350.2 6.8 %collective-permute-start.16 = (bf16[32,4,18,1]{0,2,3,1:T(8,128)(2,1)}, bf16[32,4,18,1]{0,2,3,1:T(8,128)(2,1)S(1)}, u32[]{:S(2)}, u32[]{:S(2)}) collective-permute-start(bf16[32,4,18,1]{0,2,3,1:T(8,128)(2,1)} %copy.529), channel_id=1, source_target_pairs={{0,1},{2,3},{4,5},{6,7},{8,9},{10,11},{12,13},{14,15},{16,17},{18,... | collective-permute-start | bytes 13832 | tf_op jit(solution)/shard_map/ppermute | solution.py:15
  370.0 26.1 %copy-start.22 = (f32[4,8,32,128]{3,2,1,0:T(8,128)S(1)}, f32[4,8,32,128]{3,2,1,0:T(8,128)}, u32[]{:S(2)}) copy-start(f32[4,8,32,128]{3,2,1,0:T(8,128)} %copy-done.21) | copy-start | bytes 1572868
  396.9 9.6 %collective-permute-start.18 = (bf16[32,1,16,128]{3,0,2,1:T(8,128)(2,1)S(1)}, bf16[32,1,16,128]{3,0,2,1:T(8,128)(2,1)S(1)}, u32[]{:S(2)}, u32[]{:S(2)}) collective-permute-start(bf16[32,1,16,128]{3,0,2,1:T(8,128)(2,1)S(1)} %get-tuple-element.236), channel_id=1, source_target_pairs={{0,8},{8,16},{16,24},{1,9},{9,17},{17,25},{2,10},{10,18},{18,26},{... | collective-permute-start | bytes 393224 | tf_op jit(solution)/shard_map/ppermute | solution.py:15
  398.4 8.1 %collective-permute-start.19 = (bf16[32,1,16,128]{3,0,2,1:T(8,128)(2,1)S(1)}, bf16[32,1,16,128]{3,0,2,1:T(8,128)(2,1)S(1)}, u32[]{:S(2)}, u32[]{:S(2)}) collective-permute-start(bf16[32,1,16,128]{3,0,2,1:T(8,128)(2,1)S(1)} %get-tuple-element.237), channel_id=1, source_target_pairs={{8,0},{16,8},{24,16},{9,1},{17,9},{25,17},{10,2},{18,10},{26,18},{... | collective-permute-start | bytes 393224 | tf_op jit(solution)/shard_map/ppermute | solution.py:18
  406.5 3.7 collective-permute-start.20
  408.3 4.8 collective-permute-start.21
  414.8 7.9 %collective-permute-start.23 = (bf16[32,4,18,1]{0,2,3,1:T(8,128)(2,1)S(1)}, bf16[32,4,18,1]{0,2,3,1:T(8,128)(2,1)S(1)}, u32[]{:S(2)}, u32[]{:S(2)}) collective-permute-start(bf16[32,4,18,1]{0,2,3,1:T(8,128)(2,1)S(1)} %copy.546), channel_id=1, source_target_pairs={{1,0},{3,2},{5,4},{7,6},{9,8},{11,10},{13,12},{15,14},{17,16},{19,... | collective-permute-start | bytes 13832 | tf_op jit(solution)/shard_map/ppermute | solution.py:18
  416.1 6.1 %collective-permute-start.22 = (bf16[32,4,18,1]{0,2,3,1:T(8,128)(2,1)S(1)}, bf16[32,4,18,1]{0,2,3,1:T(8,128)(2,1)S(1)}, u32[]{:S(2)}, u32[]{:S(2)}) collective-permute-start(bf16[32,4,18,1]{0,2,3,1:T(8,128)(2,1)S(1)} %copy.544), channel_id=1, source_target_pairs={{0,1},{2,3},{4,5},{6,7},{8,9},{10,11},{12,13},{14,15},{16,17},{18,... | collective-permute-start | bytes 13832 | tf_op jit(solution)/shard_map/ppermute | solution.py:15
  (130 other events, 215.1 us)
Sparse Core Ops, SparseCore 0:
  406.6 130.1 all-reduce.8
